TPU v7x, 32 devices: a whole 2x2x4 slice. The times are simulated.
32 devices in a mesh: req: 2 (over x), cand: 8 (over z, y), user: 2 (over core).
Axes of the slice: x: 2, y: 2, z: 4, core: 2. Of those that a mesh axis runs over, the one named last changes fastest.
Arguments:
- table: bfloat16 [16384, 512], P(('req', 'cand')), may hold values from -6 to 6
- hot_table: bfloat16 [256, 512], replicated, may hold values from -6 to 6
- hot_ids: int32 [256], replicated, may hold values from 0 to 16383, as said below
- hist_ids: int32 [16, 1024], P(('req', 'cand'), 'user'), may hold values from 0 to 16383, as said below
- cand_ids: int32 [16, 1024], P(('req', 'cand'), 'user'), may hold values from 0 to 16383, as said below
- w_in: bfloat16 [1, 512, 2048], replicated, may hold values from -0.25 to 0.25
- w_out: bfloat16 [1, 512, 512], replicated, may hold values from -0.25 to 0.25
- in_gain: float32 [1, 512], replicated, may hold values from 0.25 to 1.75
- attn_gain: float32 [1, 512], replicated, may hold values from 0.25 to 1.75
Outputs:
- hist_out: bfloat16 [16, 1024, 512], P(('req', 'cand'), 'user')
- cand_out: bfloat16 [16, 1024, 512], P(('req', 'cand'), 'user')
Inputs may be any that keep to these rules, and one draw needn't show every extreme that they name: `hot_ids`: distinct row ids. `hist_ids`: the owner of row id g is g // 1024, the index along req and cand together with req slowest. Of the 512 items of one device, those not in hot_ids have at most 64 items with any one owner, and one owner has exactly 64 of every device's items. `cand_ids`: of the 512 candidates of one device, those not in hot_ids have at most 48 candidates with any one owner, and one owner has exactly 48 of every device's candidates.
All inputs are finite; a program needn't handle non-finite values.
Results may differ from a plain program's by a relative error of at most 0.0055.
Values may be sent and summed in bfloat16 or wider, within the bound.
A program may use at most 64 MiB of HBM per device.

v0:
```python
import functools

import jax
import jax.numpy as jnp
from jax import lax
from jax.experimental import pallas as pl
from jax.experimental.pallas import tpu as pltpu
from jax.sharding import PartitionSpec as P

HEADS = 4
MESH = pl.DeviceIdType.MESH
F32 = jnp.float32
BF16 = jnp.bfloat16


def round_up(value, unit):
    return -(-value // unit) * unit


def silu(values):
    half = 0.5 * values
    return half + half * jnp.tanh(half)


def norm_rows(values, scale_gain):
    centred = values - jnp.mean(values, axis=-1, keepdims=True)
    variance = jnp.mean(centred * centred, axis=-1, keepdims=True)
    return centred * lax.rsqrt(variance + 1e-05) * scale_gain


def one_hot(match):
    return jnp.where(match, 1.0, 0.0).astype(BF16)


def dot(left, right):
    return jnp.dot(left, right, preferred_element_type=F32)


def divide(ids, rows_owned):
    if rows_owned & (rows_owned - 1) == 0:
        return lax.shift_right_logical(ids, jnp.int32(rows_owned.bit_length() - 1))
    return ids // rows_owned


def route(ids_row, hot_row, owners, rows_owned, cap, lane_offset):
    count = ids_row.shape[1]
    owner_lanes = round_up(owners, 128)
    column = jnp.transpose(jnp.broadcast_to(ids_row, (128, count)))[:, 0:1]
    hot_hit = jnp.where(column == hot_row, 1.0, 0.0)
    cold = 1.0 - jnp.max(hot_hit, axis=1, keepdims=True)
    owner_column = divide(column, rows_owned)
    lanes = lax.broadcasted_iota(jnp.int32, (count, owner_lanes), 1)
    member = jnp.where(owner_column == lanes, cold, 0.0)
    earlier = one_hot(
        lax.broadcasted_iota(jnp.int32, (count, count), 0)
        > lax.broadcasted_iota(jnp.int32, (count, count), 1)
    )
    before = dot(earlier, member.astype(BF16))
    rank = jnp.sum(before * member, axis=1, keepdims=True).astype(jnp.int32)
    is_cold = cold > 0.5
    slot = jnp.where(is_cold, owner_column * cap + rank, -1)
    lane_of = jnp.where(is_cold, rank + lane_offset, -1)
    placed = one_hot(lane_of == lax.broadcasted_iota(jnp.int32, (count, 128), 1))
    owner_row = divide(ids_row, rows_owned)
    number_row = ids_row - owner_row * rows_owned
    owned = owner_row == lax.broadcasted_iota(jnp.int32, (owners, count), 0)
    asks = jnp.zeros((owners, 128), F32)
    scale = 1
    while scale < rows_owned:
        digit = (lax.shift_right_logical(number_row, jnp.int32(scale.bit_length() - 1)) & 255).astype(F32)
        asks = asks + float(scale) * dot(jnp.where(owned, digit, 0.0).astype(BF16), placed)
        scale *= 256
    return slot, asks.astype(jnp.int32), hot_hit.astype(BF16)


def kernel(
    sizes,
    table_hbm,
    hot_hbm,
    hot_ids,
    hist_ids,
    cand_ids,
    w_in_hbm,
    w_out_hbm,
    in_gain,
    attn_gain,
    hist_out,
    cand_out,
    table,
    hot_table,
    w_in,
    w_out,
    ask_out,
    ask_in,
    fetch_h,
    fetch_c,
    reply_h,
    reply_c,
    keys_own,
    values_own,
    keys_other,
    values_other,
    queries,
    gate_u,
    mixed,
    embedded,
    load_sem,
    ask_send,
    ask_recv,
    h_send,
    h_recv,
    c_send,
    c_recv,
    kv_send,
    kv_recv,
    mirror_table,
    mirror_send,
    mirror_recv,
    forward_send,
    forward_recv,
):
    reqs, cands, users, cap_h, cap_c, group, pieces = sizes
    owners = reqs * cands
    half_cands = cands // 2
    near = reqs * half_cands
    rows_owned, features = table.shape
    head_dim = features // HEADS
    count_h = hist_ids.shape[1]
    count_c = cand_ids.shape[1]
    per_source = cap_h + cap_c
    my_req = lax.axis_index("req")
    my_cand = lax.axis_index("cand")
    my_user = lax.axis_index("user")
    me = my_req * cands + my_cand

    loads = [
        pltpu.make_async_copy(source, target, load_sem.at[position])
        for position, (source, target) in enumerate(
            ((table_hbm, table), (hot_hbm, hot_table), (w_in_hbm, w_in), (w_out_hbm, w_out))
        )
    ]
    for load in loads:
        load.start()

    half_start = (my_cand // half_cands) * half_cands
    far_cand = lax.rem(my_cand + half_cands, cands)

    def peer(step):
        peer_req = lax.rem(my_req + lax.rem(step, reqs), reqs)
        peer_cand = half_start + lax.rem(my_cand - half_start + step // reqs, half_cands)
        return peer_req, peer_cand

    def owner_at(req, cand, kind):
        if kind == 0:
            return req * cands + cand
        return req * cands + lax.rem(cand + half_cands, cands)

    def other_of(step, kind):
        peer_req, peer_cand = peer(step)
        return owner_at(peer_req, peer_cand, kind)

    mine = [owner_at(my_req, my_cand, kind) for kind in range(2)]

    barrier = pltpu.get_barrier_semaphore()

    @pl.loop(1, near)
    def _(step):
        peer_req, peer_cand = peer(step)
        pl.semaphore_signal(
            barrier, inc=1, device_id=(peer_req, peer_cand, my_user), device_id_type=MESH
        )

    pl.semaphore_signal(
        barrier, inc=1, device_id=(my_req, far_cand, my_user), device_id_type=MESH
    )
    for step in range(1, users):
        pl.semaphore_signal(
            barrier,
            inc=1,
            device_id=(my_req, my_cand, lax.rem(my_user + step, users)),
            device_id_type=MESH,
        )

    piece_rows = rows_owned // (users * pieces)

    def piece(number):
        start = pl.multiple_of((my_user * pieces + number) * piece_rows, piece_rows)
        return pl.ds(start, piece_rows)

    def mirror_copy(number):
        return pltpu.make_async_remote_copy(
            src_ref=table.at[piece(number)],
            dst_ref=mirror_table.at[piece(number)],
            send_sem=mirror_send.at[number],
            recv_sem=mirror_recv.at[number],
            device_id=(my_req, far_cand, my_user),
            device_id_type=MESH,
        )

    def forward_copy(number, step):
        place = number * (users - 1) + step - 1
        return pltpu.make_async_remote_copy(
            src_ref=mirror_table.at[piece(number)],
            dst_ref=mirror_table.at[piece(number)],
            send_sem=forward_send.at[place],
            recv_sem=forward_recv.at[place],
            device_id=(my_req, my_cand, lax.rem(my_user + step, users)),
            device_id_type=MESH,
        )

    hot_row = hot_ids[...]
    slot_h, asks_h, hot_h = route(hist_ids[...], hot_row, owners, rows_owned, cap_h, 0)
    loads[0].wait()
    pl.semaphore_wait(barrier, near + users - 1)
    for number in range(pieces // 2):
        mirror_copy(number).start()
    slot_c, asks_c, hot_c = route(cand_ids[...], hot_row, owners, rows_owned, cap_c, cap_h)
    asks = asks_h + asks_c
    for owner in range(owners):
        ask_out[owner] = jnp.broadcast_to(asks[owner : owner + 1], (8, 128))

    def ask_copy(step, kind):
        peer_req, peer_cand = peer(step)
        other = owner_at(peer_req, peer_cand, kind)
        return pltpu.make_async_remote_copy(
            src_ref=ask_out.at[other],
            dst_ref=ask_in.at[mine[kind]],
            send_sem=ask_send.at[other],
            recv_sem=ask_recv.at[mine[kind]],
            device_id=(peer_req, peer_cand, my_user),
            device_id_type=MESH,
        )

    def ask_arrival(other):
        return pltpu.make_async_remote_copy(
            src_ref=ask_out.at[other],
            dst_ref=ask_in.at[other],
            send_sem=ask_send.at[other],
            recv_sem=ask_recv.at[other],
            device_id=(my_req, my_cand, my_user),
            device_id_type=MESH,
        )

    def reply_copy(step, kind, fetched, replied, send_sem, recv_sem):
        peer_req, peer_cand = peer(step)
        other = owner_at(peer_req, peer_cand, kind)
        return pltpu.make_async_remote_copy(
            src_ref=fetched.at[other],
            dst_ref=replied.at[mine[kind]],
            send_sem=send_sem.at[other],
            recv_sem=recv_sem.at[mine[kind]],
            device_id=(peer_req, peer_cand, my_user),
            device_id_type=MESH,
        )

    def reply_arrival(other, fetched, replied, send_sem, recv_sem):
        return pltpu.make_async_remote_copy(
            src_ref=fetched.at[other],
            dst_ref=replied.at[other],
            send_sem=send_sem.at[other],
            recv_sem=recv_sem.at[other],
            device_id=(my_req, my_cand, my_user),
            device_id_type=MESH,
        )

    hist_reply = (fetch_h, reply_h, h_send, h_recv)
    cand_reply = (fetch_c, reply_c, c_send, c_recv)

    @pl.loop(1, near)
    def _(step):
        ask_copy(step, 0).start()

    @pl.loop(1, near)
    def _(step):
        ask_copy(step, 1).start()

    for kind in range(2):
        ask_in[mine[kind]] = ask_out[mine[kind]]

    def serve(kind, rows_of):
        @pl.loop(0, near // group)
        def _(turn):
            hits = []
            for item in range(group):
                step = turn * group + item
                other = other_of(step, kind)

                @pl.when(step > 0)
                def _():
                    ask_arrival(other).wait_recv()

                column = jnp.transpose(ask_in[other])[:per_source, 0:1]
                hits.append(
                    one_hot(column == lax.broadcasted_iota(jnp.int32, (per_source, rows_owned), 1))
                )
            fetched = dot(jnp.concatenate(hits, axis=0), rows_of[...]).astype(BF16)
            for item in range(group):
                other = other_of(turn * group + item, kind)
                start = item * per_source
                fetch_h[other] = fetched[start : start + cap_h]
                fetch_c[other] = fetched[start + cap_h : start + per_source]
            for item in range(group):
                step = turn * group + item

                @pl.when(step > 0)
                def _():
                    reply_copy(step, kind, *hist_reply).start()

        if kind == 0:
            for number in range(pieces // 2, pieces):
                mirror_copy(number).start()

        @pl.loop(1, near)
        def _(step):
            reply_copy(step, kind, *cand_reply).start()

        reply_h[mine[kind]] = fetch_h[mine[kind]]
        reply_c[mine[kind]] = fetch_c[mine[kind]]

    serve(0, table)
    for number in range(pieces):
        mirror_copy(number).wait_recv()
        for step in range(1, users):
            forward_copy(number, step).start()
    for number in range(pieces):
        for step in range(1, users):
            forward_copy(number, step).wait_recv()
    serve(1, mirror_table)

    loads[1].wait()
    loads[2].wait()
    loads[3].wait()

    def embed(slot, hot_hit, replied, cap, arrivals):
        count = slot.shape[0]
        hot_rows = dot(hot_hit, hot_table[...])
        pick = one_hot(slot == lax.broadcasted_iota(jnp.int32, (count, owners * cap), 1))

        @pl.loop(1, near)
        def _(step):
            reply_arrival(other_of(step, 0), *arrivals).wait_recv()
            reply_arrival(other_of(step, 1), *arrivals).wait_recv()

        rows = replied[...].reshape(owners * cap, features)
        embedded[...] = hot_rows + dot(pick, rows)
        return norm_rows(embedded[...], in_gain[...]).astype(BF16)

    def block(inputs, position):
        return silu(dot(inputs, w_in[:, position * features : (position + 1) * features]))

    score_scale = 1.0 / head_dim**0.5

    def attend(keys, values, mask, first):
        for head in range(HEADS):
            columns = pl.ds(head * head_dim, head_dim)
            scores = lax.dot_general(
                queries[:, columns],
                keys[:, columns],
                (((1,), (1,)), ((), ())),
                preferred_element_type=F32,
            )
            half = (scores * (0.5 * score_scale)).astype(BF16)
            weights = half + half * jnp.tanh(half)
            if mask is not None:
                weights = weights * mask
            mix = dot(weights, values[:, columns])
            if first:
                mixed[:, columns] = mix
            else:
                mixed[:, columns] += mix

    def finish():
        gated = (norm_rows(mixed[...], attn_gain[...]) * gate_u[...]).astype(BF16)
        return (embedded[...] + dot(gated, w_out[...])).astype(BF16)

    hist_in = embed(slot_h, hot_h, reply_h, cap_h, hist_reply)
    keys_own[...] = block(hist_in, 3).astype(BF16)
    values_own[...] = block(hist_in, 1).astype(BF16)
    queries[...] = block(hist_in, 2).astype(BF16)

    def kv_copies(step):
        device = (my_req, my_cand, lax.rem(my_user + step, users))
        return [
            pltpu.make_async_remote_copy(
                src_ref=source,
                dst_ref=target.at[step - 1],
                send_sem=kv_send.at[2 * (step - 1) + part],
                recv_sem=kv_recv.at[2 * (step - 1) + part],
                device_id=device,
                device_id_type=MESH,
            )
            for part, (source, target) in enumerate(
                ((keys_own, keys_other), (values_own, values_other))
            )
        ]

    sends = [copy for step in range(1, users) for copy in kv_copies(step)]
    for copy in sends:
        copy.start()
    gate_u[...] = block(hist_in, 0)
    causal = one_hot(
        lax.broadcasted_iota(jnp.int32, (count_h, count_h), 0)
        >= lax.broadcasted_iota(jnp.int32, (count_h, count_h), 1)
    )
    attend(keys_own, values_own, causal, True)
    for copy in sends:
        copy.wait_recv()
    for step in range(1, users):
        @pl.when(my_user >= step)
        def _():
            attend(keys_other.at[step - 1], values_other.at[step - 1], None, False)

    hist_out[...] = finish()

    cand_in = embed(slot_c, hot_c, reply_c, cap_c, cand_reply)
    queries[...] = block(cand_in, 2).astype(BF16)
    gate_u[...] = block(cand_in, 0)
    attend(keys_own, values_own, None, True)
    for step in range(1, users):
        attend(keys_other.at[step - 1], values_other.at[step - 1], None, False)
    cand_out[...] = finish()

    @pl.loop(1, near)
    def _(step):
        for kind in range(2):
            ask_copy(step, kind).wait_send()
            reply_copy(step, kind, *hist_reply).wait_send()
            reply_copy(step, kind, *cand_reply).wait_send()

    for number in range(pieces):
        mirror_copy(number).wait_send()
        for step in range(1, users):
            forward_copy(number, step).wait_send()

    for copy in sends:
        copy.wait_send()


def hand_out(hist_in, cand_in, hist_out, cand_out, hist_held, cand_held, in_sem, out_sem):
    inward, outward = [], []
    for source, held, target in ((hist_in, hist_held, hist_out), (cand_in, cand_held, cand_out)):
        rows = source.shape[0] // 2
        for part in range(2):
            window = pl.ds(part * rows, rows)
            place = len(inward)
            inward.append(
                pltpu.make_async_copy(source.at[window], held.at[window], in_sem.at[place])
            )
            outward.append(
                pltpu.make_async_copy(held.at[window], target.at[window], out_sem.at[place])
            )
    for copy in inward:
        copy.start()
    for arrived, leaving in zip(inward, outward):
        arrived.wait()
        leaving.start()
    for copy in outward:
        copy.wait()


def per_device(sizes, table, hot_table, hot_ids, hist_ids, cand_ids, w_in, w_out, in_gain, attn_gain):
    reqs, cands, users = sizes
    owners = reqs * cands
    rows_owned, features = table.shape
    hot_count = hot_table.shape[0]
    count_h = hist_ids.shape[1]
    count_c = cand_ids.shape[1]
    cap_h = round_up(max(2, 2 * count_h // owners), 16)
    cap_c = round_up(max(2, 3 * count_c // (2 * owners)), 16)
    near = owners // 2
    group = 4 if near % 4 == 0 else 1
    pieces = 4
    vmem = pl.BlockSpec(memory_space=pltpu.VMEM)
    anywhere = pl.BlockSpec(memory_space=pl.ANY)
    dma = pltpu.SemaphoreType.DMA
    others = max(users - 1, 1)
    hist_out, cand_out = pl.pallas_call(
        functools.partial(kernel, (reqs, cands, users, cap_h, cap_c, group, pieces)),
        out_shape=(
            jax.ShapeDtypeStruct((count_h, features), BF16),
            jax.ShapeDtypeStruct((count_c, features), BF16),
        ),
        in_specs=[anywhere, anywhere, vmem, vmem, vmem, anywhere, anywhere, vmem, vmem],
        out_specs=(vmem, vmem),
        scratch_shapes=[
            pltpu.VMEM((rows_owned, features), BF16),
            pltpu.VMEM((hot_count, features), BF16),
            pltpu.VMEM((features, 4 * features), BF16),
            pltpu.VMEM((features, features), BF16),
            pltpu.VMEM((owners, 8, 128), jnp.int32),
            pltpu.VMEM((owners, 8, 128), jnp.int32),
            pltpu.VMEM((owners, cap_h, features), BF16),
            pltpu.VMEM((owners, cap_c, features), BF16),
            pltpu.VMEM((owners, cap_h, features), BF16),
            pltpu.VMEM((owners, cap_c, features), BF16),
            pltpu.VMEM((count_h, features), BF16),
            pltpu.VMEM((count_h, features), BF16),
            pltpu.VMEM((others, count_h, features), BF16),
            pltpu.VMEM((others, count_h, features), BF16),
            pltpu.VMEM((count_h, features), BF16),
            pltpu.VMEM((count_h, features), F32),
            pltpu.VMEM((count_h, features), F32),
            pltpu.VMEM((count_h, features), F32),
            dma((4,)),
            dma((owners,)),
            dma((owners,)),
            dma((owners,)),
            dma((owners,)),
            dma((owners,)),
            dma((owners,)),
            dma((2 * others,)),
            dma((2 * others,)),
            pltpu.VMEM((rows_owned, features), BF16),
            dma((pieces,)),
            dma((pieces,)),
            dma((pieces * others,)),
            dma((pieces * others,)),
        ],
        compiler_params=pltpu.CompilerParams(collective_id=0, has_side_effects=True),
    )(
        table,
        hot_table,
        hot_ids[None],
        hist_ids,
        cand_ids,
        w_in[0],
        w_out[0],
        in_gain,
        attn_gain,
    )
    hist_out, cand_out = pl.pallas_call(
        hand_out,
        out_shape=(
            jax.ShapeDtypeStruct((count_h, features), BF16),
            jax.ShapeDtypeStruct((count_c, features), BF16),
        ),
        in_specs=[anywhere, anywhere],
        out_specs=(anywhere, anywhere),
        scratch_shapes=[
            pltpu.VMEM((count_h, features), BF16),
            pltpu.VMEM((count_c, features), BF16),
            dma((4,)),
            dma((4,)),
        ],
    )(hist_out, cand_out)
    return hist_out[None], cand_out[None]


def solution(mesh):
    sizes = tuple(mesh.shape[name] for name in ("req", "cand", "user"))
    in_specs = (
        P(("req", "cand"), None),
        P(),
        P(),
        P(("req", "cand"), "user"),
        P(("req", "cand"), "user"),
        P(),
        P(),
        P(),
        P(),
    )
    out_specs = (P(("req", "cand"), "user", None), P(("req", "cand"), "user", None))
    return jax.shard_map(
        functools.partial(per_device, sizes),
        mesh=mesh,
        in_specs=in_specs,
        out_specs=out_specs,
        check_vma=False,
    )
```

profile of v0, /device:TPU:5, one launch (start us, length us, event | category | flops | bytes accessed | tf_op | source)
XLA Modules:
  0.0 58.0 jit_solution(2275546042710561634)
XLA Ops:
  0.6 55.2 %shard_map.104 = (bf16[512,512]{1,0:T(8,128)(2,1)}, bf16[512,512]{1,0:T(8,128)(2,1)}) custom-call(bf16[1024,512]{1,0:T(8,128)(2,1)} %table_hbm.1, bf16[256,512]{1,0:T(8,128)(2,1)} %hot_hbm.1, s32[1,256]{1,0:T(1,128)} %bitcast.7, s32[1,512]{1,0:T(1,128)} %hist_ids.1, s32[1,512]{1,0:T(1,128)} %cand_ids.1, bf16[512,2048]{1,0:T(8,128)(2,1)} %bitcast.5, ...), custom_call_target="tpu_custom_call" | custom-call | tf_op jit(solution)/shard_map/pallas_call | solution.py:477
  55.8 2.0 %shard_map.105 = (bf16[512,512]{1,0:T(8,128)(2,1)}, bf16[512,512]{1,0:T(8,128)(2,1)}) custom-call(bf16[512,512]{1,0:T(8,128)(2,1)} %get-tuple-element.6.hist_in, bf16[512,512]{1,0:T(8,128)(2,1)} %get-tuple-element.7.cand_in), custom_call_target="tpu_custom_call" | custom-call | tf_op jit(solution)/shard_map/pallas_call | solution.py:531
where the time goes:
time: 58.2 us; the launch traced here: 58 us
  Pallas kernels  57.2 us (98%)
  between operations  0.8 us (1%)
    pallas_call x1, Pallas kernels, per_device(): pl.pallas_call(functools.partial(kernel, (reqs, cands, users, cap_h, cap_...  55.2 us
    pallas_call x1, Pallas kernels, per_device(): pl.pallas_call(hand_out, out_shape=(jax.ShapeDtypeStruct((count_h, featur...  1.98 us

commit v1 on v0

v1 whole, which is shorter than its diff:
```python
import functools

import jax
import jax.numpy as jnp
from jax import lax
from jax.experimental import pallas as pl
from jax.experimental.pallas import tpu as pltpu
from jax.sharding import PartitionSpec as P

HEADS = 4
PLANES = 4
MESH = pl.DeviceIdType.MESH
F32 = jnp.float32
BF16 = jnp.bfloat16


def round_up(value, unit):
    return -(-value // unit) * unit


def silu(values):
    half = 0.5 * values
    return half + half * jnp.tanh(half)


def norm_rows(values, scale_gain):
    centred = values - jnp.mean(values, axis=-1, keepdims=True)
    variance = jnp.mean(centred * centred, axis=-1, keepdims=True)
    return centred * lax.rsqrt(variance + 1e-05) * scale_gain


def one_hot(match):
    return jnp.where(match, 1.0, 0.0).astype(BF16)


def dot(left, right):
    return jnp.dot(left, right, preferred_element_type=F32)


def divide(ids, rows_owned):
    if rows_owned & (rows_owned - 1) == 0:
        return lax.shift_right_logical(ids, jnp.int32(rows_owned.bit_length() - 1))
    return ids // rows_owned


def place_of(owner, cands, width, members):
    req = divide(owner, cands)
    cand = owner - req * cands
    plane = divide(cand, width)
    return plane * members + req * width + cand - plane * width


def route(ids_row, hot_row, sizes, rows_owned, cap, lane_offset):
    owners, cands, width, members = sizes
    count = ids_row.shape[1]
    owner_lanes = round_up(owners, 128)
    column = jnp.transpose(jnp.broadcast_to(ids_row, (128, count)))[:, 0:1]
    hot_hit = jnp.where(column == hot_row, 1.0, 0.0)
    cold = 1.0 - jnp.max(hot_hit, axis=1, keepdims=True)
    place_column = place_of(divide(column, rows_owned), cands, width, members)
    lanes = lax.broadcasted_iota(jnp.int32, (count, owner_lanes), 1)
    member = jnp.where(place_column == lanes, cold, 0.0)
    earlier = one_hot(
        lax.broadcasted_iota(jnp.int32, (count, count), 0)
        > lax.broadcasted_iota(jnp.int32, (count, count), 1)
    )
    before = dot(earlier, member.astype(BF16))
    rank = jnp.sum(before * member, axis=1, keepdims=True).astype(jnp.int32)
    is_cold = cold > 0.5
    slot = jnp.where(is_cold, place_column * cap + rank, -1)
    lane_of = jnp.where(is_cold, rank + lane_offset, -1)
    placed = one_hot(lane_of == lax.broadcasted_iota(jnp.int32, (count, 128), 1))
    owner_row = divide(ids_row, rows_owned)
    number_row = ids_row - owner_row * rows_owned
    place_row = place_of(owner_row, cands, width, members)
    owned = place_row == lax.broadcasted_iota(jnp.int32, (owners, count), 0)
    asks = jnp.zeros((owners, 128), F32)
    scale = 1
    while scale < rows_owned:
        digit = (lax.shift_right_logical(number_row, jnp.int32(scale.bit_length() - 1)) & 255).astype(F32)
        asks = asks + float(scale) * dot(jnp.where(owned, digit, 0.0).astype(BF16), placed)
        scale *= 256
    return slot, asks.astype(jnp.int32), hot_hit.astype(BF16)


def kernel(
    sizes,
    table_hbm,
    hot_hbm,
    hot_ids_hbm,
    hist_ids_hbm,
    cand_ids_hbm,
    w_in_hbm,
    w_out_hbm,
    in_gain_hbm,
    attn_gain_hbm,
    hist_out,
    cand_out,
    hot_ids,
    hist_ids,
    cand_ids,
    in_gain,
    attn_gain,
    tables,
    hot_table,
    w_in,
    w_out,
    ask_out,
    ask_in,
    fetch_h,
    fetch_c,
    reply_h,
    reply_c,
    keys_own,
    values_own,
    keys_other,
    values_other,
    queries,
    gate_u,
    mixed,
    embedded_h,
    embedded_c,
    load_sem,
    ask_send,
    ask_recv,
    h_send,
    h_recv,
    c_send,
    c_recv,
    kv_send,
    kv_recv,
    mirror_send,
    mirror_recv,
    forward_send,
    forward_recv,
):
    reqs, cands, users, cap_h, cap_c, group, pieces = sizes
    owners = reqs * cands
    width = cands // PLANES
    members = reqs * width
    rows_owned, features = tables.shape[1:]
    head_dim = features // HEADS
    count_h = hist_ids.shape[1]
    per_source = cap_h + cap_c
    my_req = lax.axis_index("req")
    my_cand = lax.axis_index("cand")
    my_user = lax.axis_index("user")
    me = my_req * cands + my_cand
    plane = lax.div(my_cand, width)
    my_column = my_cand - plane * width
    my_member = my_req * width + my_column

    loads = [
        pltpu.make_async_copy(source, target, load_sem.at[position])
        for position, (source, target) in enumerate(
            (
                (hist_ids_hbm, hist_ids),
                (cand_ids_hbm, cand_ids),
                (hot_ids_hbm, hot_ids),
                (table_hbm, tables.at[0]),
                (hot_hbm, hot_table),
                (w_in_hbm, w_in),
                (w_out_hbm, w_out),
                (in_gain_hbm, in_gain),
                (attn_gain_hbm, attn_gain),
            )
        )
    ]
    for load in loads:
        load.start()

    barrier = pltpu.get_barrier_semaphore()

    @pl.loop(1, owners)
    def _(step):
        other = lax.rem(me + step, owners)
        other_req = lax.div(other, cands)
        pl.semaphore_signal(
            barrier,
            inc=1,
            device_id=(other_req, other - other_req * cands, my_user),
            device_id_type=MESH,
        )

    for step in range(1, users):
        pl.semaphore_signal(
            barrier,
            inc=1,
            device_id=(my_req, my_cand, lax.rem(my_user + step, users)),
            device_id_type=MESH,
        )

    inner = lax.rem(lax.div(plane + 1, 2), 2)
    outer = 1 - inner
    top = lax.div(plane, 3)
    facing = 3 - plane
    inner_side = 1 + top
    inner_far = 2 - top
    outer_side = 3 * (plane - 1)
    outer_far = 3 * (2 - plane)

    wanted = (
        (plane, plane, 0),
        (
            outer * facing + inner * outer_far,
            outer * facing + inner * outer_far,
            outer + 2 * inner,
        ),
        (
            outer * inner_far + inner * facing,
            outer * inner_side + inner * plane,
            outer + 2 * inner,
        ),
        (outer * inner_side + inner * outer_side, plane, 3),
    )

    def served(number):
        first = lax.div(3 - number, 3)
        last = lax.div(number, 3)
        second = lax.div(4 - number, 3) - first
        third = 1 - first - second - last
        middle = second + third
        source = (
            (first + outer * middle) * plane
            + inner * middle * facing
            + last * (outer * inner_side + inner * outer_side)
        )
        asker = (
            (first + last + inner * third) * plane
            + second * (outer * facing + inner * outer_side)
            + third * outer * inner_far
        )
        mirrored = last + inner * middle
        held = mirrored * (1 + lax.div(source - plane + 1, 2))
        return source, asker, held

    def member_at(step):
        req = lax.rem(my_req + lax.rem(step, reqs), reqs)
        column = lax.rem(my_column + lax.div(step, reqs), width)
        return req, column, req * width + column

    piece_rows = rows_owned // (users * pieces)

    def piece(number):
        start = pl.multiple_of((my_user * pieces + number) * piece_rows, piece_rows)
        return pl.ds(start, piece_rows)

    has_source = (plane > 0, plane < PLANES - 1)
    has_target = (plane < PLANES - 1, plane > 0)

    def mirror_copy(direction, number):
        place = direction * pieces + number
        target = lax.rem(my_cand + (width if direction == 0 else cands - width), cands)
        return pltpu.make_async_remote_copy(
            src_ref=tables.at[0, piece(number)],
            dst_ref=tables.at[1 + direction, piece(number)],
            send_sem=mirror_send.at[place],
            recv_sem=mirror_recv.at[place],
            device_id=(my_req, target, my_user),
            device_id_type=MESH,
        )

    def forward_copy(direction, number, step):
        place = (direction * pieces + number) * (users - 1) + step - 1
        return pltpu.make_async_remote_copy(
            src_ref=tables.at[1 + direction, piece(number)],
            dst_ref=tables.at[1 + direction, piece(number)],
            send_sem=forward_send.at[place],
            recv_sem=forward_recv.at[place],
            device_id=(my_req, my_cand, lax.rem(my_user + step, users)),
            device_id_type=MESH,
        )

    def ask_copy(entry, step):
        source, server, number = wanted[entry]
        req, column, member = member_at(step)
        return pltpu.make_async_remote_copy(
            src_ref=ask_out.at[source * members + member],
            dst_ref=ask_in.at[number * members + my_member],
            send_sem=ask_send.at[source * members + member],
            recv_sem=ask_recv.at[number * members + my_member],
            device_id=(req, server * width + column, my_user),
            device_id_type=MESH,
        )

    def ask_arrival(place):
        return pltpu.make_async_remote_copy(
            src_ref=ask_out.at[place],
            dst_ref=ask_in.at[place],
            send_sem=ask_send.at[place],
            recv_sem=ask_recv.at[place],
            device_id=(my_req, my_cand, my_user),
            device_id_type=MESH,
        )

    def reply_copy(number, step, fetched, replied, send_sem, recv_sem):
        source, asker, _ = served(number)
        req, column, member = member_at(step)
        return pltpu.make_async_remote_copy(
            src_ref=fetched.at[number * members + member],
            dst_ref=replied.at[source * members + my_member],
            send_sem=send_sem.at[number * members + member],
            recv_sem=recv_sem.at[source * members + my_member],
            device_id=(req, asker * width + column, my_user),
            device_id_type=MESH,
        )

    def reply_arrival(place, fetched, replied, send_sem, recv_sem):
        return pltpu.make_async_remote_copy(
            src_ref=fetched.at[place],
            dst_ref=replied.at[place],
            send_sem=send_sem.at[place],
            recv_sem=recv_sem.at[place],
            device_id=(my_req, my_cand, my_user),
            device_id_type=MESH,
        )

    hist_reply = (fetch_h, reply_h, h_send, h_recv)
    cand_reply = (fetch_c, reply_c, c_send, c_recv)

    def each_remote(other_plane, action):
        @pl.loop(0, members)
        def _(step):
            @pl.when((step > 0) | (other_plane != plane))
            def _():
                action(step)

    for load in loads[:3]:
        load.wait()
    hot_row = hot_ids[...]
    layout = (owners, cands, width, members)
    slot_h, asks_h, hot_h = route(hist_ids[...], hot_row, layout, rows_owned, cap_h, 0)
    slot_c, asks_c, hot_c = route(cand_ids[...], hot_row, layout, rows_owned, cap_c, cap_h)
    asks = asks_h + asks_c
    for owner in range(owners):
        ask_out[owner] = jnp.broadcast_to(asks[owner : owner + 1], (8, 128))
    loads[3].wait()
    pl.semaphore_wait(barrier, owners + users - 2)

    for entry in (1, 2):
        each_remote(wanted[entry][1], lambda step: ask_copy(entry, step).start())
    for number in range(pieces):
        for direction in range(2):

            @pl.when(has_target[direction])
            def _():
                mirror_copy(direction, number).start()

    for entry in (0, 3):
        each_remote(wanted[entry][1], lambda step: ask_copy(entry, step).start())

    for source, server, number in wanted:

        @pl.when(server == plane)
        def _():
            ask_in[number * members + my_member] = ask_out[source * members + my_member]

    def start_replies(number, reply):
        each_remote(
            served(number)[1], lambda step: reply_copy(number, step, *reply).start()
        )

    def serve(start, stop, reply, first, rows, ready):
        fetched, replied = reply[:2]

        @pl.loop(start, stop)
        def _(number):
            source, asker, held = served(number)

            @pl.loop(0, members // group)
            def _(turn):
                hits = []
                for item in range(group):
                    step = turn * group + item
                    place = number * members + member_at(step)[2]

                    if first == 0:

                        @pl.when((step > 0) | (asker != plane))
                        def _():
                            ask_arrival(place).wait_recv()

                    column = jnp.transpose(ask_in[place])[first : first + rows, 0:1]
                    hits.append(
                        one_hot(column == lax.broadcasted_iota(jnp.int32, (rows, rows_owned), 1))
                    )
                found = dot(jnp.concatenate(hits, axis=0), tables[held]).astype(BF16)
                for item in range(group):
                    place = number * members + member_at(turn * group + item)[2]
                    fetched[place] = found[item * rows : (item + 1) * rows]

            @pl.when(number >= ready)
            def _():
                start_replies(number, reply)

            @pl.when(asker == plane)
            def _():
                replied[source * members + my_member] = fetched[number * members + my_member]

    early = 1 + 2 * outer
    serve(0, early, hist_reply, 0, cap_h, PLANES)
    start_replies(0, hist_reply)
    serve(0, early, cand_reply, cap_h, cap_c, PLANES)
    start_replies(0, cand_reply)

    loads[4].wait()
    embedded_h[...] = dot(hot_h, hot_table[...])
    embedded_c[...] = dot(hot_c, hot_table[...])

    for number in range(pieces):
        if number == pieces - 1:
            for sent in range(pieces):
                for direction in range(2):

                    @pl.when(has_target[direction])
                    def _():
                        mirror_copy(direction, sent).wait_send()

            @pl.loop(1, early)
            def _(number):
                start_replies(number, hist_reply)

        for direction in range(2):

            @pl.when(has_source[direction])
            def _():
                mirror_copy(direction, number).wait_recv()
                for step in range(1, users):
                    forward_copy(direction, number, step).start()

    for number in range(pieces):
        for direction in range(2):
            for step in range(1, users):

                @pl.when(has_source[direction])
                def _():
                    forward_copy(direction, number, step).wait_recv()

    serve(early, PLANES, hist_reply, 0, cap_h, early)
    serve(early, PLANES, cand_reply, cap_h, cap_c, PLANES)

    for load in loads[5:]:
        load.wait()

    def gather(entries, slot, embedded, cap, arrivals):
        count = slot.shape[0]
        replied = arrivals[1]
        for entry in entries:
            source, server, _ = wanted[entry]
            offset = source * (members * cap)
            pick = one_hot(
                slot - offset == lax.broadcasted_iota(jnp.int32, (count, members * cap), 1)
            )
            each_remote(
                server,
                lambda step: reply_arrival(
                    source * members + member_at(step)[2], *arrivals
                ).wait_recv(),
            )
            rows = replied[pl.ds(source * members, members)]
            embedded[...] += dot(pick, rows.reshape(members * cap, features))

    def normed(embedded):
        return norm_rows(embedded[...], in_gain[...]).astype(BF16)

    def block(inputs, position):
        return silu(dot(inputs, w_in[:, position * features : (position + 1) * features]))

    score_scale = 1.0 / head_dim**0.5

    def attend(keys, values, mask, first):
        for head in range(HEADS):
            columns = pl.ds(head * head_dim, head_dim)
            scores = lax.dot_general(
                queries[:, columns],
                keys[:, columns],
                (((1,), (1,)), ((), ())),
                preferred_element_type=F32,
            )
            half = (scores * (0.5 * score_scale)).astype(BF16)
            weights = half + half * jnp.tanh(half)
            if mask is not None:
                weights = weights * mask
            mix = dot(weights, values[:, columns])
            if first:
                mixed[:, columns] = mix
            else:
                mixed[:, columns] += mix

    def finish(embedded):
        gated = (norm_rows(mixed[...], attn_gain[...]) * gate_u[...]).astype(BF16)
        return (embedded[...] + dot(gated, w_out[...])).astype(BF16)

    gather((0,), slot_h, embedded_h, cap_h, hist_reply)

    @pl.loop(0, PLANES)
    def _(number):
        each_remote(
            served(number)[1], lambda step: reply_copy(number, step, *hist_reply).wait_send()
        )

    @pl.loop(1, PLANES)
    def _(number):
        start_replies(number, cand_reply)

    gather((3, 2, 1), slot_h, embedded_h, cap_h, hist_reply)
    hist_in = normed(embedded_h)
    keys_own[...] = block(hist_in, 3).astype(BF16)
    values_own[...] = block(hist_in, 1).astype(BF16)
    queries[...] = block(hist_in, 2).astype(BF16)

    def kv_copies(step):
        device = (my_req, my_cand, lax.rem(my_user + step, users))
        return [
            pltpu.make_async_remote_copy(
                src_ref=source,
                dst_ref=target.at[step - 1],
                send_sem=kv_send.at[2 * (step - 1) + part],
                recv_sem=kv_recv.at[2 * (step - 1) + part],
                device_id=device,
                device_id_type=MESH,
            )
            for part, (source, target) in enumerate(
                ((keys_own, keys_other), (values_own, values_other))
            )
        ]

    sends = [copy for step in range(1, users) for copy in kv_copies(step)]
    for copy in sends:
        copy.start()
    gate_u[...] = block(hist_in, 0)
    causal = one_hot(
        lax.broadcasted_iota(jnp.int32, (count_h, count_h), 0)
        >= lax.broadcasted_iota(jnp.int32, (count_h, count_h), 1)
    )
    attend(keys_own, values_own, causal, True)
    for copy in sends:
        copy.wait_recv()
    for step in range(1, users):
        @pl.when(my_user >= step)
        def _():
            attend(keys_other.at[step - 1], values_other.at[step - 1], None, False)

    hist_out[...] = finish(embedded_h)

    gather((0, 3, 2, 1), slot_c, embedded_c, cap_c, cand_reply)
    cand_in = normed(embedded_c)
    queries[...] = block(cand_in, 2).astype(BF16)
    gate_u[...] = block(cand_in, 0)
    attend(keys_own, values_own, None, True)
    for step in range(1, users):
        attend(keys_other.at[step - 1], values_other.at[step - 1], None, False)
    cand_out[...] = finish(embedded_c)

    for entry in range(PLANES):
        each_remote(wanted[entry][1], lambda step: ask_copy(entry, step).wait_send())

    @pl.loop(0, PLANES)
    def _(number):
        asker = served(number)[1]
        each_remote(asker, lambda step: reply_copy(number, step, *cand_reply).wait_send())

    for number in range(pieces):
        for direction in range(2):

            @pl.when(has_source[direction])
            def _():
                for step in range(1, users):
                    forward_copy(direction, number, step).wait_send()

    for copy in sends:
        copy.wait_send()


def hand_out(hist_in, cand_in, hist_out, cand_out, out_sem):
    outward = [
        pltpu.make_async_copy(source, target, out_sem.at[place])
        for place, (source, target) in enumerate(((hist_in, hist_out), (cand_in, cand_out)))
    ]
    for copy in outward:
        copy.start()
    for copy in outward:
        copy.wait()


def per_device(sizes, table, hot_table, hot_ids, hist_ids, cand_ids, w_in, w_out, in_gain, attn_gain):
    reqs, cands, users = sizes
    owners = reqs * cands
    rows_owned, features = table.shape
    hot_count = hot_table.shape[0]
    count_h = hist_ids.shape[1]
    count_c = cand_ids.shape[1]
    cap_h = round_up(max(2, 2 * count_h // owners), 16)
    cap_c = round_up(max(2, 3 * count_c // (2 * owners)), 16)
    members = owners // PLANES
    group = 4 if members % 4 == 0 else 1
    pieces = 4
    vmem = pl.BlockSpec(memory_space=pltpu.VMEM)
    anywhere = pl.BlockSpec(memory_space=pl.ANY)
    dma = pltpu.SemaphoreType.DMA
    others = max(users - 1, 1)
    given = (
        table,
        hot_table,
        hot_ids[None],
        hist_ids,
        cand_ids,
        w_in[0],
        w_out[0],
        in_gain,
        attn_gain,
    )
    hist_out, cand_out = pl.pallas_call(
        functools.partial(kernel, (reqs, cands, users, cap_h, cap_c, group, pieces)),
        out_shape=(
            pltpu.VMEM((count_h, features), BF16),
            pltpu.VMEM((count_c, features), BF16),
        ),
        in_specs=[anywhere] * len(given),
        out_specs=(vmem, vmem),
        scratch_shapes=[
            pltpu.VMEM((1, hot_count), jnp.int32),
            pltpu.VMEM((1, count_h), jnp.int32),
            pltpu.VMEM((1, count_c), jnp.int32),
            pltpu.VMEM((1, features), F32),
            pltpu.VMEM((1, features), F32),
            pltpu.VMEM((3, rows_owned, features), BF16),
            pltpu.VMEM((hot_count, features), BF16),
            pltpu.VMEM((features, 4 * features), BF16),
            pltpu.VMEM((features, features), BF16),
            pltpu.VMEM((owners, 8, 128), jnp.int32),
            pltpu.VMEM((owners, 8, 128), jnp.int32),
            pltpu.VMEM((owners, cap_h, features), BF16),
            pltpu.VMEM((owners, cap_c, features), BF16),
            pltpu.VMEM((owners, cap_h, features), BF16),
            pltpu.VMEM((owners, cap_c, features), BF16),
            pltpu.VMEM((count_h, features), BF16),
            pltpu.VMEM((count_h, features), BF16),
            pltpu.VMEM((others, count_h, features), BF16),
            pltpu.VMEM((others, count_h, features), BF16),
            pltpu.VMEM((count_h, features), BF16),
            pltpu.VMEM((count_h, features), F32),
            pltpu.VMEM((count_h, features), F32),
            pltpu.VMEM((count_h, features), F32),
            pltpu.VMEM((count_c, features), F32),
            dma((len(given),)),
            dma((owners,)),
            dma((owners,)),
            dma((owners,)),
            dma((owners,)),
            dma((owners,)),
            dma((owners,)),
            dma((2 * others,)),
            dma((2 * others,)),
            dma((2 * pieces,)),
            dma((2 * pieces,)),
            dma((2 * pieces * others,)),
            dma((2 * pieces * others,)),
        ],
        compiler_params=pltpu.CompilerParams(
            collective_id=0, has_side_effects=True, vmem_limit_bytes=44 * 1024 * 1024
        ),
    )(*(pltpu.with_memory_space_constraint(array, pltpu.HBM) for array in given))
    hist_out, cand_out = pl.pallas_call(
        hand_out,
        out_shape=(
            jax.ShapeDtypeStruct((count_h, features), BF16),
            jax.ShapeDtypeStruct((count_c, features), BF16),
        ),
        in_specs=[vmem, vmem],
        out_specs=(anywhere, anywhere),
        scratch_shapes=[dma((2,))],
        compiler_params=pltpu.CompilerParams(vmem_limit_bytes=16 * 1024 * 1024),
    )(hist_out, cand_out)
    return hist_out[None], cand_out[None]


def solution(mesh):
    sizes = tuple(mesh.shape[name] for name in ("req", "cand", "user"))
    in_specs = (
        P(("req", "cand"), None),
        P(),
        P(),
        P(("req", "cand"), "user"),
        P(("req", "cand"), "user"),
        P(),
        P(),
        P(),
        P(),
    )
    out_specs = (P(("req", "cand"), "user", None), P(("req", "cand"), "user", None))
    return jax.shard_map(
        functools.partial(per_device, sizes),
        mesh=mesh,
        in_specs=in_specs,
        out_specs=out_specs,
        check_vma=False,
    )
```

time: 58.2 us -> 50 us (0.86)
  the two profiles are of different devices: /device:TPU:5 before, /device:TPU:0 now
where the time goes in v1:
time: 50 us; the launch traced here: 49.8 us
  Pallas kernels  49 us (98%)
  between operations  0.8 us (2%)
    pallas_call x1, Pallas kernels, per_device(): pl.pallas_call(functools.partial(kernel, (reqs, cands, users, cap_h, cap_...  48 us

profile of v1, /device:TPU:0, one launch (start us, length us, event | category | flops | bytes accessed | tf_op | source)
XLA Modules:
  0.0 49.8 jit_solution(6367010393296146150)
XLA Ops:
  0.6 48.0 %shard_map.104 = (bf16[512,512]{1,0:T(8,128)(2,1)S(1)}, bf16[512,512]{1,0:T(8,128)(2,1)S(1)}) custom-call(bf16[1024,512]{1,0:T(8,128)(2,1)} %table_hbm.1, bf16[256,512]{1,0:T(8,128)(2,1)} %hot_hbm.1, s32[1,256]{1,0:T(1,128)} %bitcast.7, s32[1,512]{1,0:T(1,128)} %hist_ids_hbm.1, s32[1,512]{1,0:T(1,128)} %cand_ids_hbm.1, bf16[512,2048]{1,0:T(8,128)(2,1)} %bitcast.5, ...), custom_call_target="tpu_custom_call" | custom-call | tf_op jit(solution)/shard_map/pallas_call | solution.py:613
  48.7 1.0 %shard_map.105 = (bf16[512,512]{1,0:T(8,128)(2,1)}, bf16[512,512]{1,0:T(8,128)(2,1)}) custom-call(bf16[512,512]{1,0:T(8,128)(2,1)S(1)} %get-tuple-element.6.hist_in, bf16[512,512]{1,0:T(8,128)(2,1)S(1)} %get-tuple-element.7.cand_in), custom_call_target="tpu_custom_call" | custom-call | tf_op jit(solution)/shard_map/pallas_call | solution.py:664

commit v2 on v1

--- a/solution.py
+++ b/solution.py
@@ -239,7 +239,9 @@
         column = lax.rem(my_column + lax.div(step, reqs), width)
         return req, column, req * width + column
 
-    piece_rows = rows_owned // (users * pieces)
+    half_rows = rows_owned // users
+    own_half = pl.multiple_of(my_user * half_rows, half_rows)
+    piece_rows = half_rows // pieces
 
     def piece(number):
         start = pl.multiple_of((my_user * pieces + number) * piece_rows, piece_rows)
@@ -254,14 +256,14 @@
         return pltpu.make_async_remote_copy(
             src_ref=tables.at[0, piece(number)],
             dst_ref=tables.at[1 + direction, piece(number)],
-            send_sem=mirror_send.at[place],
+            send_sem=mirror_send.at[direction],
             recv_sem=mirror_recv.at[place],
             device_id=(my_req, target, my_user),
             device_id_type=MESH,
         )
 
     def forward_copy(direction, number, step):
-        place = (direction * pieces + number) * (users - 1) + step - 1
+        place = direction * (users - 1) + step - 1
         return pltpu.make_async_remote_copy(
             src_ref=tables.at[1 + direction, piece(number)],
             dst_ref=tables.at[1 + direction, piece(number)],
@@ -277,21 +279,36 @@
         return pltpu.make_async_remote_copy(
             src_ref=ask_out.at[source * members + member],
             dst_ref=ask_in.at[number * members + my_member],
-            send_sem=ask_send.at[source * members + member],
-            recv_sem=ask_recv.at[number * members + my_member],
+            send_sem=ask_send.at[0],
+            recv_sem=ask_recv.at[number],
             device_id=(req, server * width + column, my_user),
             device_id_type=MESH,
         )
 
-    def ask_arrival(place):
+    def batch(held, start, count, send_sem, recv_sem):
+        window = held.at[pl.ds(start, count)]
         return pltpu.make_async_remote_copy(
-            src_ref=ask_out.at[place],
-            dst_ref=ask_in.at[place],
-            send_sem=ask_send.at[place],
-            recv_sem=ask_recv.at[place],
+            src_ref=window,
+            dst_ref=window,
+            send_sem=send_sem,
+            recv_sem=recv_sem,
             device_id=(my_req, my_cand, my_user),
             device_id_type=MESH,
         )
+
+    def each_batch(other_plane, action):
+        @pl.when(other_plane != plane)
+        def _():
+            action(members)
+
+        if members > 1:
+
+            @pl.when(other_plane == plane)
+            def _():
+                action(members - 1)
+
+    def asks_arrival(number, count):
+        return batch(ask_in, number * members, count, ask_send.at[0], ask_recv.at[number])
 
     def reply_copy(number, step, fetched, replied, send_sem, recv_sem):
         source, asker, _ = served(number)
@@ -299,21 +316,17 @@
         return pltpu.make_async_remote_copy(
             src_ref=fetched.at[number * members + member],
             dst_ref=replied.at[source * members + my_member],
-            send_sem=send_sem.at[number * members + member],
-            recv_sem=recv_sem.at[source * members + my_member],
+            send_sem=send_sem.at[number],
+            recv_sem=recv_sem.at[source],
             device_id=(req, asker * width + column, my_user),
             device_id_type=MESH,
         )
 
-    def reply_arrival(place, fetched, replied, send_sem, recv_sem):
-        return pltpu.make_async_remote_copy(
-            src_ref=fetched.at[place],
-            dst_ref=replied.at[place],
-            send_sem=send_sem.at[place],
-            recv_sem=recv_sem.at[place],
-            device_id=(my_req, my_cand, my_user),
-            device_id_type=MESH,
-        )
+    def replies_sent(number, count, fetched, replied, send_sem, recv_sem):
+        return batch(fetched, number * members, count, send_sem.at[number], recv_sem.at[number])
+
+    def replies_arrival(source, count, fetched, replied, send_sem, recv_sem):
+        return batch(replied, source * members, count, send_sem.at[source], recv_sem.at[source])
 
     hist_reply = (fetch_h, reply_h, h_send, h_recv)
     cand_reply = (fetch_c, reply_c, c_send, c_recv)
@@ -324,6 +337,18 @@
             @pl.when((step > 0) | (other_plane != plane))
             def _():
                 action(step)
+
+    def start_tables(first, last):
+        for number in range(first, last):
+            for direction in range(2):
+
+                @pl.when(has_target[direction])
+                def _():
+                    mirror_copy(direction, number).start()
+
+    loads[3].wait()
+    pl.semaphore_wait(barrier, owners + users - 2)
+    start_tables(0, 1)
 
     for load in loads[:3]:
         load.wait()
@@ -334,18 +359,9 @@
     asks = asks_h + asks_c
     for owner in range(owners):
         ask_out[owner] = jnp.broadcast_to(asks[owner : owner + 1], (8, 128))
-    loads[3].wait()
-    pl.semaphore_wait(barrier, owners + users - 2)
-
     for entry in (1, 2):
         each_remote(wanted[entry][1], lambda step: ask_copy(entry, step).start())
-    for number in range(pieces):
-        for direction in range(2):
-
-            @pl.when(has_target[direction])
-            def _():
-                mirror_copy(direction, number).start()
-
+    start_tables(1, pieces)
     for entry in (0, 3):
         each_remote(wanted[entry][1], lambda step: ask_copy(entry, step).start())
 
@@ -366,6 +382,8 @@
         @pl.loop(start, stop)
         def _(number):
             source, asker, held = served(number)
+            if first == 0:
+                each_batch(asker, lambda count: asks_arrival(number, count).wait_recv())
 
             @pl.loop(0, members // group)
             def _(turn):
@@ -373,12 +391,6 @@
                 for item in range(group):
                     step = turn * group + item
                     place = number * members + member_at(step)[2]
-
-                    if first == 0:
-
-                        @pl.when((step > 0) | (asker != plane))
-                        def _():
-                            ask_arrival(place).wait_recv()
 
                     column = jnp.transpose(ask_in[place])[first : first + rows, 0:1]
                     hits.append(
@@ -409,12 +421,13 @@
 
     for number in range(pieces):
         if number == pieces - 1:
-            for sent in range(pieces):
-                for direction in range(2):
-
-                    @pl.when(has_target[direction])
-                    def _():
-                        mirror_copy(direction, sent).wait_send()
+            for direction in range(2):
+
+                @pl.when(has_target[direction])
+                def _():
+                    batch(
+                        tables.at[0], own_half, half_rows, mirror_send.at[direction], mirror_recv.at[0]
+                    ).wait_send()
 
             @pl.loop(1, early)
             def _(number):
@@ -428,13 +441,18 @@
                 for step in range(1, users):
                     forward_copy(direction, number, step).start()
 
-    for number in range(pieces):
-        for direction in range(2):
-            for step in range(1, users):
-
-                @pl.when(has_source[direction])
-                def _():
-                    forward_copy(direction, number, step).wait_recv()
+    def forwarded(direction, step):
+        place = direction * (users - 1) + step - 1
+        return batch(
+            tables.at[1 + direction], own_half, half_rows, forward_send.at[place], forward_recv.at[place]
+        )
+
+    for direction in range(2):
+        for step in range(1, users):
+
+            @pl.when(has_source[direction])
+            def _():
+                forwarded(direction, step).wait_recv()
 
     serve(early, PLANES, hist_reply, 0, cap_h, early)
     serve(early, PLANES, cand_reply, cap_h, cap_c, PLANES)
@@ -451,11 +469,8 @@
             pick = one_hot(
                 slot - offset == lax.broadcasted_iota(jnp.int32, (count, members * cap), 1)
             )
-            each_remote(
-                server,
-                lambda step: reply_arrival(
-                    source * members + member_at(step)[2], *arrivals
-                ).wait_recv(),
+            each_batch(
+                server, lambda count: replies_arrival(source, count, *arrivals).wait_recv()
             )
             rows = replied[pl.ds(source * members, members)]
             embedded[...] += dot(pick, rows.reshape(members * cap, features))
@@ -495,13 +510,27 @@
 
     @pl.loop(0, PLANES)
     def _(number):
-        each_remote(
-            served(number)[1], lambda step: reply_copy(number, step, *hist_reply).wait_send()
+        each_batch(
+            served(number)[1], lambda count: replies_sent(number, count, *hist_reply).wait_send()
         )
 
     @pl.loop(1, PLANES)
     def _(number):
         start_replies(number, cand_reply)
+
+    for local, here in ((2, outer), (3, inner)):
+
+        @pl.when(here == 1)
+        def _():
+            count = PLANES * members - local
+            batch(ask_out, 0, count, ask_send.at[0], ask_recv.at[0]).wait_send()
+
+    for direction in range(2):
+        for step in range(1, users):
+
+            @pl.when(has_source[direction])
+            def _():
+                forwarded(direction, step).wait_send()
 
     gather((3, 2, 1), slot_h, embedded_h, cap_h, hist_reply)
     hist_in = normed(embedded_h)
@@ -552,24 +581,14 @@
         attend(keys_other.at[step - 1], values_other.at[step - 1], None, False)
     cand_out[...] = finish(embedded_c)
 
-    for entry in range(PLANES):
-        each_remote(wanted[entry][1], lambda step: ask_copy(entry, step).wait_send())
+    for copy in sends:
+        copy.wait_send()
 
     @pl.loop(0, PLANES)
     def _(number):
-        asker = served(number)[1]
-        each_remote(asker, lambda step: reply_copy(number, step, *cand_reply).wait_send())
-
-    for number in range(pieces):
-        for direction in range(2):
-
-            @pl.when(has_source[direction])
-            def _():
-                for step in range(1, users):
-                    forward_copy(direction, number, step).wait_send()
-
-    for copy in sends:
-        copy.wait_send()
+        each_batch(
+            served(number)[1], lambda count: replies_sent(number, count, *cand_reply).wait_send()
+        )
 
 
 def hand_out(hist_in, cand_in, hist_out, cand_out, out_sem):
@@ -644,18 +663,18 @@
             pltpu.VMEM((count_h, features), F32),
             pltpu.VMEM((count_c, features), F32),
             dma((len(given),)),
-            dma((owners,)),
-            dma((owners,)),
-            dma((owners,)),
-            dma((owners,)),
-            dma((owners,)),
-            dma((owners,)),
+            dma((1,)),
+            dma((PLANES,)),
+            dma((PLANES,)),
+            dma((PLANES,)),
+            dma((PLANES,)),
+            dma((PLANES,)),
             dma((2 * others,)),
             dma((2 * others,)),
+            dma((2,)),
             dma((2 * pieces,)),
-            dma((2 * pieces,)),
-            dma((2 * pieces * others,)),
-            dma((2 * pieces * others,)),
+            dma((2 * others,)),
+            dma((2 * others,)),
         ],
         compiler_params=pltpu.CompilerParams(
             collective_id=0, has_side_effects=True, vmem_limit_bytes=44 * 1024 * 1024

time: 50 us -> 47.3 us (0.946)
  Pallas kernels: 49 us -> 46.4 us
    pallas_call x1, Pallas kernels: 48 us -> 45.4 us  [per_device(): pl.pallas_call(functools.partial(kernel, (reqs, cands, users, cap_h, cap_...]
where the time goes in v2:
time: 47.3 us; the launch traced here: 47.2 us
  Pallas kernels  46.4 us (98%)
  between operations  0.8 us (2%)
    pallas_call x1, Pallas kernels, per_device(): pl.pallas_call(functools.partial(kernel, (reqs, cands, users, cap_h, cap_...  45.4 us
    pallas_call x1, Pallas kernels, per_device(): pl.pallas_call(hand_out, out_shape=(jax.ShapeDtypeStruct((count_h, featur...  0.99 us

profile of v2, /device:TPU:0, one launch (start us, length us, event | category | flops | bytes accessed | tf_op | source)
XLA Modules:
  0.0 47.2 jit_solution(2654284887911974265)
XLA Ops:
  0.6 45.4 %shard_map.104 = (bf16[512,512]{1,0:T(8,128)(2,1)S(1)}, bf16[512,512]{1,0:T(8,128)(2,1)S(1)}) custom-call(bf16[1024,512]{1,0:T(8,128)(2,1)} %table_hbm.1, bf16[256,512]{1,0:T(8,128)(2,1)} %hot_hbm.1, s32[1,256]{1,0:T(1,128)} %bitcast.7, s32[1,512]{1,0:T(1,128)} %hist_ids_hbm.1, s32[1,512]{1,0:T(1,128)} %cand_ids_hbm.1, bf16[512,2048]{1,0:T(8,128)(2,1)} %bitcast.5, ...), custom_call_target="tpu_custom_call" | custom-call | tf_op jit(solution)/shard_map/pallas_call | solution.py:632
  46.0 1.0 %shard_map.105 = (bf16[512,512]{1,0:T(8,128)(2,1)}, bf16[512,512]{1,0:T(8,128)(2,1)}) custom-call(bf16[512,512]{1,0:T(8,128)(2,1)S(1)} %get-tuple-element.6.hist_in, bf16[512,512]{1,0:T(8,128)(2,1)S(1)} %get-tuple-element.7.cand_in), custom_call_target="tpu_custom_call" | custom-call | tf_op jit(solution)/shard_map/pallas_call | solution.py:683

commit v3 on v2

--- a/solution.py
+++ b/solution.py
@@ -483,12 +483,12 @@
 
     score_scale = 1.0 / head_dim**0.5
 
-    def attend(keys, values, mask, first):
+    def attend(keys, values, mask, first, rows=slice(None), kept=slice(None)):
         for head in range(HEADS):
             columns = pl.ds(head * head_dim, head_dim)
             scores = lax.dot_general(
-                queries[:, columns],
-                keys[:, columns],
+                queries[rows, columns],
+                keys[kept, columns],
                 (((1,), (1,)), ((), ())),
                 preferred_element_type=F32,
             )
@@ -496,11 +496,11 @@
             weights = half + half * jnp.tanh(half)
             if mask is not None:
                 weights = weights * mask
-            mix = dot(weights, values[:, columns])
+            mix = dot(weights, values[kept, columns])
             if first:
-                mixed[:, columns] = mix
+                mixed[rows, columns] = mix
             else:
-                mixed[:, columns] += mix
+                mixed[rows, columns] += mix
 
     def finish(embedded):
         gated = (norm_rows(mixed[...], attn_gain[...]) * gate_u[...]).astype(BF16)
@@ -534,10 +534,6 @@
 
     gather((3, 2, 1), slot_h, embedded_h, cap_h, hist_reply)
     hist_in = normed(embedded_h)
-    keys_own[...] = block(hist_in, 3).astype(BF16)
-    values_own[...] = block(hist_in, 1).astype(BF16)
-    queries[...] = block(hist_in, 2).astype(BF16)
-
     def kv_copies(step):
         device = (my_req, my_cand, lax.rem(my_user + step, users))
         return [
@@ -554,15 +550,23 @@
             )
         ]
 
-    sends = [copy for step in range(1, users) for copy in kv_copies(step)]
-    for copy in sends:
-        copy.start()
+    copies = [kv_copies(step) for step in range(1, users)]
+    keys_own[...] = block(hist_in, 3).astype(BF16)
+    for keys_copy, _ in copies:
+        keys_copy.start()
+    values_own[...] = block(hist_in, 1).astype(BF16)
+    for _, values_copy in copies:
+        values_copy.start()
+    sends = [copy for pair in copies for copy in pair]
+    queries[...] = block(hist_in, 2).astype(BF16)
     gate_u[...] = block(hist_in, 0)
     causal = one_hot(
         lax.broadcasted_iota(jnp.int32, (count_h, count_h), 0)
         >= lax.broadcasted_iota(jnp.int32, (count_h, count_h), 1)
     )
-    attend(keys_own, values_own, causal, True)
+    half = count_h // 2
+    attend(keys_own, values_own, causal[:half, :half], True, slice(0, half), slice(0, half))
+    attend(keys_own, values_own, causal[half:], True, slice(half, count_h))
     for copy in sends:
         copy.wait_recv()
     for step in range(1, users):

time: 47.3 us -> 47.3 us (level)
  no operation moved by 1% of the time
where the time goes in v3:
time: 47.3 us; the launch traced here: 47.2 us
  Pallas kernels  46.4 us (98%)
  between operations  0.8 us (2%)
    pallas_call x1, Pallas kernels, per_device(): pl.pallas_call(functools.partial(kernel, (reqs, cands, users, cap_h, cap_...  45.4 us
    pallas_call x1, Pallas kernels, per_device(): pl.pallas_call(hand_out, out_shape=(jax.ShapeDtypeStruct((count_h, featur...  0.99 us

profile of v3, /device:TPU:0, one launch (start us, length us, event | category | flops | bytes accessed | tf_op | source)
XLA Modules:
  0.0 47.2 jit_solution(9764886677305175283)
XLA Ops:
  0.6 45.4 %shard_map.104 = (bf16[512,512]{1,0:T(8,128)(2,1)S(1)}, bf16[512,512]{1,0:T(8,128)(2,1)S(1)}) custom-call(bf16[1024,512]{1,0:T(8,128)(2,1)} %table_hbm.1, bf16[256,512]{1,0:T(8,128)(2,1)} %hot_hbm.1, s32[1,256]{1,0:T(1,128)} %bitcast.7, s32[1,512]{1,0:T(1,128)} %hist_ids_hbm.1, s32[1,512]{1,0:T(1,128)} %cand_ids_hbm.1, bf16[512,2048]{1,0:T(8,128)(2,1)} %bitcast.5, ...), custom_call_target="tpu_custom_call" | custom-call | tf_op jit(solution)/shard_map/pallas_call | solution.py:636
  46.0 1.0 %shard_map.105 = (bf16[512,512]{1,0:T(8,128)(2,1)}, bf16[512,512]{1,0:T(8,128)(2,1)}) custom-call(bf16[512,512]{1,0:T(8,128)(2,1)S(1)} %get-tuple-element.6.hist_in, bf16[512,512]{1,0:T(8,128)(2,1)S(1)} %get-tuple-element.7.cand_in), custom_call_target="tpu_custom_call" | custom-call | tf_op jit(solution)/shard_map/pallas_call | solution.py:687
